TPU v7x, 32 devices: a whole 2x2x4 slice. The times are simulated.
32 devices in a mesh: seq: 8 (over z, y), head: 4 (over x, core).
Axes of the slice: x: 2, y: 2, z: 4, core: 2. Of those that a mesh axis runs over, the one named last changes fastest.
Arguments:
- doc_lengths: int32 [32], P(('seq', 'head')), may hold values from 1 to 2688, 6144 in all
- queries: bfloat16 [6144, 8192], P('seq', 'head'), may hold values from -24 to 24
- key_states: bfloat16 [6144, 1024], P('seq', 'head'), may hold values from -24 to 24
- value_states: bfloat16 [6144, 1024], P('seq', 'head'), may hold values from -6 to 6
Outputs:
- attended: bfloat16 [6144, 8192], P('seq', 'head')
Inputs may be any that keep to these rules, and one draw needn't show every extreme that they name: `doc_lengths`: the 32 lengths sum to 6144; the largest is exactly 2688.
All inputs are finite; a program needn't handle non-finite values. No bound on the sum of `doc_lengths` on one device may be relied on, other than what follows from the above.
Results may differ from a plain program's by a relative error of at most 0.0028.
Values may be sent and summed in bfloat16 or wider, within the bound.
A program may use at most 64 MiB of HBM per device.

v0:
```python
import functools
import math

import jax
import jax.numpy as jnp
from jax import lax
from jax.experimental import pallas as pl
from jax.experimental.pallas import tpu as pltpu
from jax.sharding import PartitionSpec as P

HD = 128
TILE = 128
LONGEST = 2688
STEP = 512
CHUNK = 256
AHEAD = 2
DIGIT = 32
NO_KEY = HD - 1
BIG = float(2**20)
MESH = pl.DeviceIdType.MESH

VIA_EVEN = (0, 1)
VIA_ODD = (0,)


def attend(
    n_seq,
    n_head,
    kv_heads,
    group,
    lens_ref,
    q_ref,
    k_ref,
    v_ref,
    out_ref,
    lens,
    qv,
    kv,
    qt,
    kf,
    qf,
    digit_a,
    digit_b,
    acc,
    m_ref,
    l_ref,
    out_v,
    lens_send,
    lens_recv,
    in_sems,
    q_sems,
    send_sems,
    recv_sems,
    out_sems,
):
    rows = k_ref.shape[0]
    pieces = rows // TILE
    back = pl.cdiv(LONGEST, rows)
    kept = (LONGEST - (back - 1) * rows) // TILE
    kv_width = kv_heads * HD
    width = group * TILE
    n_chunks = width // CHUNK
    own = back * rows
    first_key = own - LONGEST
    per = lens_ref.shape[0]

    seq = lax.axis_index("seq")
    head = lax.axis_index("head")
    count = n_seq * n_head
    me = seq * n_head + head
    odd = seq % 2
    is_even = odd == 0
    is_odd = odd == 1

    def device(flat):
        return (flat // n_head, flat % n_head)

    own_rows = pl.ds(own, rows)
    load_k = pltpu.make_async_copy(k_ref, kv.at[own_rows, pl.ds(0, kv_width)], in_sems.at[0])
    load_v = pltpu.make_async_copy(
        v_ref, kv.at[own_rows, pl.ds(kv_width, kv_width)], in_sems.at[1]
    )
    load_lens = pltpu.make_async_copy(lens_ref, lens.at[pl.ds(me * per, per)], in_sems.at[2])
    load_k.start()
    load_v.start()
    load_lens.start()
    load_q = [
        pltpu.make_async_copy(
            q_ref.at[pl.ds(t * TILE, TILE)], qv.at[pl.ds(t * TILE, TILE)], q_sems.at[t]
        )
        for t in range(pieces)
    ]
    for copy in load_q:
        copy.start()

    barrier = pltpu.get_barrier_semaphore()

    def greet(i, carry):
        pl.semaphore_signal(
            barrier, inc=1, device_id=device((me + i) % count), device_id_type=MESH
        )
        return carry

    lax.fori_loop(1, count, greet, 0)

    for rel in range(1, back + 1):
        @pl.when(seq < rel)
        def _():
            begin = own - rel * rows
            skip = 0 if rel < back else (pieces - kept) * TILE
            kv[begin + skip : begin + rows, :] = jnp.zeros((rows - skip, 2 * kv_width), kv.dtype)

    load_k.wait()
    load_v.wait()
    load_lens.wait()
    pl.semaphore_wait(barrier, count - 1)

    def lens_copy(slot, i):
        return pltpu.make_async_remote_copy(
            src_ref=lens.at[pl.ds(slot * per, per)],
            dst_ref=lens.at[pl.ds(slot * per, per)],
            send_sem=lens_send.at[i],
            recv_sem=lens_recv.at[slot],
            device_id=device((me + i) % count),
            device_id_type=MESH,
        )

    def send_lens(i, carry):
        lens_copy(me, i).start()
        return carry

    lax.fori_loop(1, count, send_lens, 0)

    def place(rel, j):
        return kv.at[pl.ds(own - rel * rows + j * TILE, TILE), :]

    def hop(kind, rel_here, rel_there, j, to):
        return pltpu.make_async_remote_copy(
            src_ref=place(rel_here, j),
            dst_ref=place(rel_there, j),
            send_sem=send_sems.at[kind, j],
            recv_sem=recv_sems.at[rel_there, j],
            device_id=(to, head),
            device_id_type=MESH,
        )

    hi = range(pieces - kept, pieces)
    every = range(pieces)
    sends = [
        (0, 0, 2, every, seq + 2, seq + 2 < n_seq),
        (1, 0, 1, every, seq + 1, is_even),
        (2, 2, 3, [j for j in every if j not in VIA_ODD], seq + 1, is_even & (seq >= 2)),
        (3, 2, 1, every, seq - 1, is_odd & (seq >= 2)),
        (4, 2, 4, hi, seq + 2, is_even & (seq >= 2) & (seq + 2 < n_seq)),
        (
            5,
            2,
            4,
            [j for j in every if j in hi or j not in VIA_EVEN],
            seq + 2,
            is_odd & (seq >= 2) & (seq + 2 < n_seq),
        ),
        (6, 1, 3, VIA_EVEN, seq + 2, is_even & (seq >= 2) & (seq + 2 < n_seq)),
        (7, 1, 3, VIA_ODD, seq + 2, is_odd & (seq + 2 < n_seq)),
        (
            8,
            4,
            3,
            [j for j in every if j not in VIA_EVEN],
            seq - 1,
            is_odd & (seq >= 4),
        ),
    ]

    def start_sends(rel, j):
        for kind, here, there, chunks, to, condition in sends:
            if here == rel and j in chunks:
                @pl.when(condition)
                def _():
                    hop(kind, here, there, j, to).start()

    def arrive(rel, j):
        if rel == 4 and j not in hi:
            if j in VIA_EVEN:
                return
            condition = is_odd & (seq >= rel)
        else:
            condition = seq >= rel

        @pl.when(condition)
        def _():
            hop(0, rel, rel, j, (seq + 1) % n_seq).wait_recv()

        start_sends(rel, j)

    for j in every:
        start_sends(0, j)

    for t in range(pieces):
        load_q[t].wait()

    def turn(t, carry):
        for c in range(kv_heads):
            for g in range(group):
                tile = qv[pl.ds(pl.multiple_of(t * TILE, TILE), TILE), pl.ds((c * group + g) * HD, HD)]
                qt[c, :, pl.ds(pl.multiple_of(t * width, TILE) + g * TILE, TILE)] = tile.T
        return carry

    lax.fori_loop(0, pieces, turn, 0)

    def wait_lens(i, carry):
        lens_copy((me + i) % count, i).wait_recv()
        return carry

    lax.fori_loop(1, count, wait_lens, 0)

    n_groups = digit_a.shape[0]
    position = (
        (seq - back) * rows
        + lax.broadcasted_iota(jnp.int32, (n_groups, TILE), 0) * TILE
        + lax.broadcasted_iota(jnp.int32, (n_groups, TILE), 1)
    )

    def count_ends(d, carry):
        end, ids = carry
        end = end + lens[d]
        return end, ids + jnp.where(position >= end, 1, 0)

    _, ids = lax.fori_loop(
        0,
        count * per,
        count_ends,
        (jnp.zeros((1, TILE), jnp.int32), jnp.zeros((n_groups, TILE), jnp.int32)),
    )
    digit_a[...] = jnp.where(position < 0, NO_KEY, DIGIT + ids // DIGIT)
    digit_b[...] = jnp.where(position < 0, NO_KEY, ids % DIGIT)

    feature = lax.broadcasted_iota(jnp.int32, (HD, TILE), 0)

    def match(g):
        return (feature == digit_a[pl.ds(g, 1), :]) | (feature == digit_b[pl.ds(g, 1), :])

    def key_features(g, carry):
        one_hot = jnp.where(match(g), 1.0, 0.0).astype(jnp.bfloat16)
        kf[pl.ds(pl.multiple_of(g * TILE, TILE), TILE), :] = one_hot.T
        return carry

    lax.fori_loop(first_key // TILE, (own + rows) // TILE, key_features, 0)

    def query_features(t, carry):
        away = jnp.where(match(own // TILE + t), 0.0, -BIG).astype(jnp.bfloat16)
        for i in range(CHUNK // TILE):
            qf[:, pl.ds(pl.multiple_of(t * CHUNK, TILE) + i * TILE, TILE)] = away
        return carry

    lax.fori_loop(0, pieces, query_features, 0)

    scale = math.log2(math.e) / math.sqrt(HD)

    def block(t, begin, n_keys, first):
        flags = kf[pl.ds(begin, n_keys), :]
        marks = qf[:, pl.ds(pl.multiple_of(t * CHUNK, TILE), CHUNK)]
        keys, values = [], []
        for c in range(kv_heads):
            keys.append(
                jnp.concatenate([kv[pl.ds(begin, n_keys), pl.ds(c * HD, HD)], flags], axis=1)
            )
            values.append(kv[pl.ds(begin, n_keys), pl.ds(kv_width + c * HD, HD)].T)
        if first:
            tail = 2 * TILE
            key_row = begin + n_keys - tail + lax.broadcasted_iota(jnp.int32, (tail, CHUNK), 0)
            query_row = own + t * TILE + lax.broadcasted_iota(jnp.int32, (tail, CHUNK), 1) % TILE
            later = key_row > query_row
        units = [(c, i) for c in range(kv_heads) for i in range(n_chunks)]

        def lanes(i):
            return pl.ds(pl.multiple_of(t * width, TILE) + i * CHUNK, CHUNK)

        def score(unit):
            c, i = unit
            queries = jnp.concatenate([qt[c, :, lanes(i)], marks], axis=0)
            return jnp.dot(keys[c], queries, preferred_element_type=jnp.float32)

        ready = [score(unit) for unit in units[:AHEAD]]
        for at, (c, i) in enumerate(units):
            if at + AHEAD < len(units):
                ready.append(score(units[at + AHEAD]))
            scores = ready.pop(0)
            if first:
                end = jnp.where(later, -BIG, scores[n_keys - tail :])
                scores = jnp.concatenate([scores[: n_keys - tail], end], axis=0) if n_keys > tail else end
            top = jnp.max(scores, axis=0, keepdims=True)
            if first:
                new_max = top
            else:
                old_max = m_ref[c, :, lanes(i)]
                new_max = jnp.maximum(old_max, top)
            weights = jnp.exp2((scores - new_max) * scale)
            part_sum = jnp.sum(weights.reshape(n_keys // 8, 8, CHUNK), axis=0)
            update = jnp.dot(
                values[c], weights.astype(jnp.bfloat16), preferred_element_type=jnp.float32
            )
            if first:
                l_ref[c, :, lanes(i)] = part_sum
                acc[c, :, lanes(i)] = update
            else:
                shrink = jnp.exp2((old_max - new_max) * scale)
                l_ref[c, :, lanes(i)] = l_ref[c, :, lanes(i)] * shrink + part_sum
                acc[c, :, lanes(i)] = acc[c, :, lanes(i)] * shrink + update
            m_ref[c, :, lanes(i)] = new_max

    events = [[(2, 0)], [(2, 1)], [(2, 2), (2, 3)]]
    for pair in range(pieces // 2):
        def own_tile(t, carry):
            block(t, own, (pair + 1) * 2 * TILE, True)
            return carry

        lax.fori_loop(2 * pair, 2 * pair + 2, own_tile, 0)
        for rel, j in events[min(pair, 2)]:
            arrive(rel, j)

    mid_events = {
        2: [(1, 0), (1, 1)],
        4: [(2, 4)],
        5: [(1, 2), (2, 5)],
        8: [(4, 2), (1, 3)],
        10: [(1, 4), (4, 3)],
        11: [(1, 5)],
        13: [(4, 4)],
        15: [(4, 5)],
        17: [(3, 2), (3, 3), (3, 4), (3, 5)],
    }
    mid_begin = own - 2 * rows

    def mid(it, carry):
        block(it % pieces, pl.multiple_of(mid_begin + (it // pieces) * STEP, TILE), STEP, False)
        for at, arrivals in mid_events.items():
            @pl.when(it == at)
            def _():
                for rel, j in arrivals:
                    arrive(rel, j)
        return carry

    lax.fori_loop(0, 3 * pieces, mid, 0)

    def far(it, carry):
        block(
            it % pieces, pl.multiple_of(mid_begin - STEP - (it // pieces) * STEP, TILE), STEP, False
        )
        @pl.when(it == 0)
        def _():
            for rel, j in [(3, 0), (3, 1)]:
                arrive(rel, j)
        return carry

    lax.fori_loop(0, pieces + 4, far, 0)

    block(0, first_key, TILE, False)
    block(4, first_key + 4 * TILE, TILE, False)

    def finish(t, carry):
        for c in range(kv_heads):
            for g in range(group):
                lanes = pl.ds(pl.multiple_of(t * width, TILE) + g * TILE, TILE)
                total = jnp.sum(l_ref[c, :, lanes], axis=0, keepdims=True)
                result = acc[c, :, lanes] * (1.0 / total)
                out_v[pl.ds(pl.multiple_of(t * TILE, TILE), TILE), pl.ds((c * group + g) * HD, HD)] = (
                    result.T.astype(jnp.bfloat16)
                )
        tile_rows = pl.ds(pl.multiple_of(t * TILE, TILE), TILE)
        pltpu.make_async_copy(out_v.at[tile_rows], out_ref.at[tile_rows], out_sems.at[t]).start()
        return carry

    lax.fori_loop(0, pieces, finish, 0)

    for kind, here, there, chunks, to, condition in sends:
        @pl.when(condition)
        def _():
            for j in chunks:
                hop(kind, here, there, j, to).wait_send()

    def drain_lens(i, carry):
        lens_copy(me, i).wait_send()
        return carry

    lax.fori_loop(1, count, drain_lens, 0)

    def drain_out(t, carry):
        tile_rows = pl.ds(pl.multiple_of(t * TILE, TILE), TILE)
        pltpu.make_async_copy(out_v.at[tile_rows], out_ref.at[tile_rows], out_sems.at[t]).wait()
        return carry

    lax.fori_loop(0, pieces, drain_out, 0)


def body(n_seq, n_head, doc_lengths, queries, key_states, value_states):
    rows, q_width = queries.shape
    pieces = rows // TILE
    kv_heads = key_states.shape[1] // HD
    group = q_width // (kv_heads * HD)
    back = pl.cdiv(LONGEST, rows)
    window = (back + 1) * rows
    per = doc_lengths.shape[0]
    count = n_seq * n_head
    columns = pieces * group * TILE
    lens = jnp.broadcast_to(doc_lengths[:, None, None], (per, 1, TILE))
    kernel = functools.partial(attend, n_seq, n_head, kv_heads, group)
    return pl.pallas_call(
        kernel,
        out_shape=jax.ShapeDtypeStruct(queries.shape, jnp.bfloat16),
        in_specs=[pl.BlockSpec(memory_space=pl.ANY)] * 4,
        out_specs=pl.BlockSpec(memory_space=pl.ANY),
        scratch_shapes=[
            pltpu.VMEM((count * per, 1, TILE), jnp.int32),
            pltpu.VMEM((rows, q_width), jnp.bfloat16),
            pltpu.VMEM((window, 2 * kv_heads * HD), jnp.bfloat16),
            pltpu.VMEM((kv_heads, HD, columns), jnp.bfloat16),
            pltpu.VMEM((window, HD), jnp.bfloat16),
            pltpu.VMEM((HD, pieces * CHUNK), jnp.bfloat16),
            pltpu.VMEM((window // TILE, TILE), jnp.int32),
            pltpu.VMEM((window // TILE, TILE), jnp.int32),
            pltpu.VMEM((kv_heads, HD, columns), jnp.float32),
            pltpu.VMEM((kv_heads, 1, columns), jnp.float32),
            pltpu.VMEM((kv_heads, 8, columns), jnp.float32),
            pltpu.VMEM((rows, q_width), jnp.bfloat16),
            pltpu.SemaphoreType.DMA((count,)),
            pltpu.SemaphoreType.DMA((count,)),
            pltpu.SemaphoreType.DMA((3,)),
            pltpu.SemaphoreType.DMA((pieces,)),
            pltpu.SemaphoreType.DMA((9, pieces)),
            pltpu.SemaphoreType.DMA((back + 1, pieces)),
            pltpu.SemaphoreType.DMA((pieces,)),
        ],
        compiler_params=pltpu.CompilerParams(
            collective_id=0, has_side_effects=True, vmem_limit_bytes=56 * 1024 * 1024
        ),
    )(lens, queries, key_states, value_states)


def solution(mesh):
    return jax.shard_map(
        functools.partial(body, mesh.shape["seq"], mesh.shape["head"]),
        mesh=mesh,
        in_specs=(P(("seq", "head")), P("seq", "head"), P("seq", "head"), P("seq", "head")),
        out_specs=P("seq", "head"),
        check_vma=False,
    )
```

profile of v0, /device:TPU:16, one launch (start us, length us, event | category | flops | bytes accessed | tf_op | source)
XLA Modules:
  0.0 84.6 jit_solution(11726874721124792222)
XLA Ops:
  0.7 0.5 broadcast_in_dim.9.lens_ref
  1.1 79.4 %shard_map.46 = bf16[768,2048]{1,0:T(8,128)(2,1)} custom-call(s32[1,1,128]{2,1,0:T(1,128)} %broadcast_in_dim.9.lens_ref, bf16[768,2048]{1,0:T(8,128)(2,1)} %q_ref.1, bf16[768,256]{1,0:T(8,128)(2,1)} %k_ref.1, bf16[768,256]{1,0:T(8,128)(2,1)} %v_ref.1), custom_call_target="tpu_custom_call" | custom-call | tf_op jit(solution)/shard_map/pallas_call | solution.py:408
  80.6 4.0 %copy.7 = bf16[768,2048]{1,0:T(8,128)(2,1)} copy(bf16[768,2048]{1,0:T(8,128)(2,1)} %shard_map.46) | data formatting | bytes 6291456
where the time goes:
time: 86 us; the launch traced here: 84.6 us
  Pallas kernels  79.4 us (92%)
  local copies, waits for them, and re-layouts  4.45 us (5%)
    pallas_call x1, Pallas kernels, body(): pl.pallas_call(kernel, out_shape=jax.ShapeDtypeStruct(queries.shape, jnp....  79.4 us
    unnamed x1, local copies, waits for them, and re-layouts  3.97 us

commit v1 on v0

v1 whole, which is shorter than its diff:
```python
import functools
import math

import jax
import jax.numpy as jnp
from jax import lax
from jax.experimental import pallas as pl
from jax.experimental.pallas import tpu as pltpu
from jax.sharding import PartitionSpec as P

HD = 128
TILE = 128
LONGEST = 2688
CHUNK = 256
SLOTS = 8
PS = 2
DIGIT = 32
NO_KEY = HD - 1
BIG = float(2**20)
MESH = pl.DeviceIdType.MESH

VIA_EVEN = (0, 1)
VIA_ODD = (0,)


def attend(
    n_seq,
    n_head,
    kv_heads,
    group,
    lens_ref,
    q_ref,
    k_ref,
    v_ref,
    out_ref,
    lens,
    qv,
    kv,
    qt,
    kf,
    qf,
    digit_a,
    digit_b,
    acc,
    m_ref,
    s_buf,
    p_buf,
    m_now,
    shrink,
    lens_send,
    lens_recv,
    in_sems,
    q_sems,
    send_sems,
    recv_sems,
):
    rows = k_ref.shape[0]
    pieces = rows // TILE
    back = pl.cdiv(LONGEST, rows)
    kept = (LONGEST - (back - 1) * rows) // TILE
    kv_width = kv_heads * HD
    width = group * TILE
    n_chunks = width // CHUNK
    own = back * rows
    first_key = own - LONGEST
    per = lens_ref.shape[0]

    seq = lax.axis_index("seq")
    head = lax.axis_index("head")
    count = n_seq * n_head
    me = seq * n_head + head
    odd = seq % 2
    is_even = odd == 0
    is_odd = odd == 1

    own_rows = pl.ds(own, rows)
    load_k = pltpu.make_async_copy(k_ref, kv.at[own_rows, pl.ds(0, kv_width)], in_sems.at[0])
    load_v = pltpu.make_async_copy(
        v_ref, kv.at[own_rows, pl.ds(kv_width, kv_width)], in_sems.at[1]
    )
    load_k.start()
    load_v.start()
    load_q = [
        pltpu.make_async_copy(
            q_ref.at[pl.ds(t * TILE, TILE)], qv.at[pl.ds(t * TILE, TILE)], q_sems.at[t]
        )
        for t in range(pieces)
    ]
    for copy in load_q:
        copy.start()

    barrier = pltpu.get_barrier_semaphore()
    offsets = [(a, b) for a in range(n_seq) for b in range(n_head) if a or b]

    def peer(offset):
        return ((seq + offset[0]) % n_seq, (head + offset[1]) % n_head)

    for offset in offsets:
        pl.semaphore_signal(barrier, inc=1, device_id=peer(offset), device_id_type=MESH)

    for i in range(per):
        lens[me * per + i] = jnp.full((1, TILE), lens_ref[i], jnp.int32)

    for rel in range(1, back + 1):
        @pl.when(seq < rel)
        def _():
            begin = own - rel * rows
            skip = 0 if rel < back else (pieces - kept) * TILE
            kv[begin + skip : begin + rows, :] = jnp.zeros((rows - skip, 2 * kv_width), kv.dtype)

    load_k.wait()
    load_v.wait()
    pl.semaphore_wait(barrier, count - 1)

    def lens_copy(slot, i):
        return pltpu.make_async_remote_copy(
            src_ref=lens.at[pl.ds(slot * per, per)],
            dst_ref=lens.at[pl.ds(slot * per, per)],
            send_sem=lens_send.at[i],
            recv_sem=lens_recv.at[slot],
            device_id=peer(offsets[i]),
            device_id_type=MESH,
        )

    def place(rel, j):
        return kv.at[pl.ds(own - rel * rows + j * TILE, TILE), :]

    def hop(kind, rel_here, rel_there, j, to):
        return pltpu.make_async_remote_copy(
            src_ref=place(rel_here, j),
            dst_ref=place(rel_there, j),
            send_sem=send_sems.at[kind, j],
            recv_sem=recv_sems.at[rel_there, j],
            device_id=(to, head),
            device_id_type=MESH,
        )

    hi = range(pieces - kept, pieces)
    every = range(pieces)
    sends = [
        (0, 0, 2, every, seq + 2, seq + 2 < n_seq),
        (1, 0, 1, every, seq + 1, is_even),
        (2, 2, 3, [j for j in every if j not in VIA_ODD], seq + 1, is_even & (seq >= 2)),
        (3, 2, 1, every, seq - 1, is_odd & (seq >= 2)),
        (4, 2, 4, hi, seq + 2, is_even & (seq >= 2) & (seq + 2 < n_seq)),
        (
            5,
            2,
            4,
            [j for j in every if j in hi or j not in VIA_EVEN],
            seq + 2,
            is_odd & (seq >= 2) & (seq + 2 < n_seq),
        ),
        (6, 1, 3, VIA_EVEN, seq + 2, is_even & (seq >= 2) & (seq + 2 < n_seq)),
        (7, 1, 3, VIA_ODD, seq + 2, is_odd & (seq + 2 < n_seq)),
        (
            8,
            4,
            3,
            [j for j in every if j not in VIA_EVEN],
            seq - 1,
            is_odd & (seq >= 4),
        ),
    ]

    def start_sends(rel, j):
        for kind, here, there, chunks, to, condition in sends:
            if here == rel and j in chunks:
                @pl.when(condition)
                def _():
                    hop(kind, here, there, j, to).start()

    def arrive(rel, j):
        if rel == 4 and j not in hi:
            if j in VIA_EVEN:
                return
            condition = is_odd & (seq >= rel)
        else:
            condition = seq >= rel

        @pl.when(condition)
        def _():
            hop(0, rel, rel, j, (seq + 1) % n_seq).wait_recv()

        start_sends(rel, j)

    for i in range(count - 1):
        lens_copy(me, i).start()
    for j in every:
        start_sends(0, j)

    for t in range(pieces):
        load_q[t].wait()

    def turn(t, carry):
        for c in range(kv_heads):
            for g in range(group):
                tile = qv[pl.ds(pl.multiple_of(t * TILE, TILE), TILE), pl.ds((c * group + g) * HD, HD)]
                qt[c, :, pl.ds(pl.multiple_of(t * width, TILE) + g * TILE, TILE)] = tile.T
        return carry

    lax.fori_loop(0, pieces, turn, 0)

    for i in range(count - 1):
        there = peer(offsets[i])
        lens_copy(there[0] * n_head + there[1], i).wait_recv()

    n_groups = digit_a.shape[0]
    position = (
        (seq - back) * rows
        + lax.broadcasted_iota(jnp.int32, (n_groups, TILE), 0) * TILE
        + lax.broadcasted_iota(jnp.int32, (n_groups, TILE), 1)
    )

    ends_step = 8

    def count_ends(k, carry):
        end, ids = carry
        for i in range(ends_step):
            end = end + lens[k * ends_step + i]
            ids = ids + jnp.where(position >= end, 1, 0)
        return end, ids

    _, ids = lax.fori_loop(
        0,
        count * per // ends_step,
        count_ends,
        (jnp.zeros((1, TILE), jnp.int32), jnp.zeros((n_groups, TILE), jnp.int32)),
    )
    digit_a[...] = jnp.where(position < 0, NO_KEY, DIGIT + ids // DIGIT)
    digit_b[...] = jnp.where(position < 0, NO_KEY, ids % DIGIT)

    feature = lax.broadcasted_iota(jnp.int32, (HD, TILE), 0)

    def match(g):
        return (feature == digit_a[g : g + 1, :]) | (feature == digit_b[g : g + 1, :])

    def key_features(g):
        one_hot = jnp.where(match(g), 1.0, 0.0).astype(jnp.bfloat16)
        kf[g * TILE : (g + 1) * TILE, :] = one_hot.T

    for t in range(pieces):
        key_features(own // TILE + t)
        away = jnp.where(match(own // TILE + t), 0.0, -BIG).astype(jnp.bfloat16)
        for i in range(CHUNK // TILE):
            qf[:, t * CHUNK + i * TILE : t * CHUNK + (i + 1) * TILE] = away

    scale = math.log2(math.e) / math.sqrt(HD)
    units = [(a, c, i) for a in range(2) for c in range(kv_heads) for i in range(n_chunks)]
    one = len(units) // 2
    slots = s_buf.shape[0]
    ahead = slots - 1

    def lanes(t, i):
        return pl.ds(pl.multiple_of(t * width, TILE) + i * CHUNK, CHUNK)

    def scores(k, u, t, slabs, first):
        a, c, i = units[u]
        t = t + a
        marks = qf[:, pl.ds(pl.multiple_of(t * CHUNK, TILE), CHUNK)]
        keys = jnp.concatenate(
            [
                jnp.concatenate([kv[pl.ds(at, n), pl.ds(c * HD, HD)], kf[pl.ds(at, n), :]], axis=1)
                for at, n in slabs
            ],
            axis=0,
        )
        queries = jnp.concatenate([qt[c, :, lanes(t, i)], marks], axis=0)
        result = jnp.dot(keys, queries, preferred_element_type=jnp.float32)
        n_keys = result.shape[0]
        if first:
            key = lax.broadcasted_iota(jnp.int32, (TILE, CHUNK), 0)
            query = lax.broadcasted_iota(jnp.int32, (TILE, CHUNK), 1) % TILE
            end = jnp.where(key > query, -BIG, result[n_keys - TILE :])
            result = jnp.concatenate([result[: n_keys - TILE], end], axis=0) if n_keys > TILE else end
        s_buf[k % slots, :n_keys, :] = result
        top = jnp.max(result, axis=0, keepdims=True)
        if not first:
            old_max = m_ref[c, :, lanes(t, i)]
            top = jnp.maximum(old_max, top)
            shrink[k % len(units)] = jnp.exp2((old_max - top) * scale)
        m_now[k % len(units)] = top
        m_ref[c, :, lanes(t, i)] = top

    def weigh(k, u, t, n_keys, first):
        a, c, i = units[u]
        t = t + a
        top = m_now[k % len(units)]
        for r in range(0, n_keys, TILE):
            weights = jnp.exp2((s_buf[k % slots, r : r + TILE, :] - top) * scale)
            p_buf[k % PS, r : r + TILE, :] = weights.astype(jnp.bfloat16)

    def add_values(k, u, t, slabs, first):
        a, c, i = units[u]
        t = t + a
        values = jnp.concatenate(
            [kv[pl.ds(at, n), pl.ds(kv_width + c * HD, HD)].T for at, n in slabs], axis=1
        )
        n_keys = values.shape[1]
        values = jnp.concatenate([values, jnp.ones((16, n_keys), values.dtype)], axis=0)
        weights = p_buf[k % PS, :n_keys, :]
        update = jnp.dot(values, weights, preferred_element_type=jnp.float32)[: HD + 8]
        if first:
            acc[c, :, lanes(t, i)] = update
        else:
            acc[c, :, lanes(t, i)] = acc[c, :, lanes(t, i)] * shrink[k % len(units)] + update

    earlier = list(range(first_key // TILE, own // TILE))
    share = pl.cdiv(len(earlier), pieces - 1)
    events = {2: [(2, 0)], pieces - 2: [(2, 1)], pieces - 1: [(2, 2), (2, 3)]}
    items = [(t, u) for t in range(pieces) for u in range(one)]

    def item(k):
        t, u = items[k]
        return u, t, [(own, (t + 1) * TILE)]

    for k in range(ahead):
        scores(k, *item(k), True)
    for k, (t, u) in enumerate(items):
        if k + ahead < len(items):
            scores(k + ahead, *item(k + ahead), True)
        if k:
            add_values(k - 1, *item(k - 1), True)
        weigh(k, u, t, (t + 1) * TILE, True)
        if u == one - 1:
            for g in earlier[t * share : (t + 1) * share]:
                key_features(g)
            for rel, j in events.get(t, []):
                arrive(rel, j)
    add_values(len(items) - 1, *item(len(items) - 1), True)

    n_step = 4 * TILE
    pairs = pieces // 2
    steps = 5 * pairs - 1

    def where(it):
        it = it + it // (4 * pairs - 1)
        stage = it // pairs
        begin = own - 2 * rows + (stage - stage // 3 * 5) * n_step
        return 2 * (it % pairs), [(pl.multiple_of(begin, TILE), n_step)]

    step_events = {
        0: [(1, 0)],
        1: [(1, 1)],
        2: [(2, 4), (2, 5)],
        3: [(1, 2)],
        4: [(1, 3), (4, 2)],
        5: [(1, 4), (1, 5), (4, 3)],
        6: [(4, 4)],
        7: [(4, 5)],
        8: [(3, 0), (3, 1)],
        10: [(3, 2), (3, 3), (3, 4), (3, 5)],
    }

    def hook(it):
        for low in (0, 4, 8):
            @pl.when(it // 4 == low // 4)
            def _():
                for at, arrivals in step_events.items():
                    if low <= at < low + 4:
                        @pl.when(it == at)
                        def _():
                            for rel, j in arrivals:
                                arrive(rel, j)

    n_units = len(units)
    last = n_units - 1
    for u in range(ahead):
        scores(u, u, *where(0), False)
    p_buf[last % PS] = jnp.zeros(p_buf.shape[1:], p_buf.dtype)
    shrink[last] = jnp.ones((1, CHUNK), jnp.float32)

    def step(it, carry):
        hook(it)
        now, then = where(it), where(it + 1 - (it + 1) // steps)
        before = where(it - (it + steps - 1) // steps)
        for u in range(n_units):
            later = u + ahead
            scores(later, later % n_units, *(now if later < n_units else then), False)
            add_values(u - 1, (u - 1) % n_units, *(now if u else before), False)
            weigh(u, u, now[0], n_step, False)
        return carry

    lax.fori_loop(0, steps, step, 0)
    add_values(last, last, *where(steps - 1), False)

    def finish(t):
        for c in range(kv_heads):
            for g in range(group):
                at = slice(t * width + g * TILE, t * width + (g + 1) * TILE)
                result = (acc[c, :HD, at] * (1.0 / acc[c, HD : HD + 1, at])).astype(jnp.bfloat16)
                columns = slice((c * group + g) * HD, (c * group + g + 1) * HD)
                out_ref[t * TILE : (t + 1) * TILE, columns] = result.T

    ends = [(0, first_key), (4, first_key + n_step)]
    items = [(t, u, [(at, TILE)]) for t, at in ends for u in range(one)]
    others = [t for t in range(pieces) if t not in (0, 4)]
    for k, (t, u, slabs) in enumerate(items[:ahead]):
        scores(k, u, t, slabs, False)
    for k, (t, u, slabs) in enumerate(items):
        if k + ahead < len(items):
            scores(k + ahead, *[items[k + ahead][i] for i in (1, 0, 2)], False)
        weigh(k, u, t, TILE, False)
        add_values(k, u, t, slabs, False)
        if k % 2 and k // 2 < len(others):
            finish(others[k // 2])
    finish(0)
    finish(4)

    for kind, here, there, chunks, to, condition in sends:
        @pl.when(condition)
        def _():
            for j in chunks:
                hop(kind, here, there, j, to).wait_send()

    for i in range(count - 1):
        lens_copy(me, i).wait_send()


def body(n_seq, n_head, doc_lengths, queries, key_states, value_states):
    rows, q_width = queries.shape
    pieces = rows // TILE
    kv_heads = key_states.shape[1] // HD
    group = q_width // (kv_heads * HD)
    back = pl.cdiv(LONGEST, rows)
    window = (back + 1) * rows
    per = doc_lengths.shape[0]
    count = n_seq * n_head
    columns = pieces * group * TILE
    units = 2 * kv_heads * group * TILE // CHUNK
    kernel = functools.partial(attend, n_seq, n_head, kv_heads, group)
    return pl.pallas_call(
        kernel,
        out_shape=pltpu.VMEM(queries.shape, jnp.bfloat16),
        in_specs=[pl.BlockSpec(memory_space=pltpu.SMEM)]
        + [pl.BlockSpec(memory_space=pl.ANY)] * 3,
        out_specs=pl.BlockSpec(memory_space=pltpu.VMEM),
        scratch_shapes=[
            pltpu.VMEM((count * per, 1, TILE), jnp.int32),
            pltpu.VMEM((rows, q_width), jnp.bfloat16),
            pltpu.VMEM((window, 2 * kv_heads * HD), jnp.bfloat16),
            pltpu.VMEM((kv_heads, HD, columns), jnp.bfloat16),
            pltpu.VMEM((window, HD), jnp.bfloat16),
            pltpu.VMEM((HD, pieces * CHUNK), jnp.bfloat16),
            pltpu.VMEM((window // TILE, TILE), jnp.int32),
            pltpu.VMEM((window // TILE, TILE), jnp.int32),
            pltpu.VMEM((kv_heads, HD + 8, columns), jnp.float32),
            pltpu.VMEM((kv_heads, 1, columns), jnp.float32),
            pltpu.VMEM((SLOTS, rows, CHUNK), jnp.float32),
            pltpu.VMEM((PS, rows, CHUNK), jnp.bfloat16),
            pltpu.VMEM((units, 1, CHUNK), jnp.float32),
            pltpu.VMEM((units, 1, CHUNK), jnp.float32),
            pltpu.SemaphoreType.DMA((count,)),
            pltpu.SemaphoreType.DMA((count,)),
            pltpu.SemaphoreType.DMA((2,)),
            pltpu.SemaphoreType.DMA((pieces,)),
            pltpu.SemaphoreType.DMA((9, pieces)),
            pltpu.SemaphoreType.DMA((back + 1, pieces)),
        ],
        compiler_params=pltpu.CompilerParams(
            collective_id=0, has_side_effects=True, vmem_limit_bytes=56 * 1024 * 1024
        ),
    )(doc_lengths, queries, key_states, value_states)


def solution(mesh):
    return jax.shard_map(
        functools.partial(body, mesh.shape["seq"], mesh.shape["head"]),
        mesh=mesh,
        in_specs=(P(("seq", "head")), P("seq", "head"), P("seq", "head"), P("seq", "head")),
        out_specs=P("seq", "head"),
        check_vma=False,
    )
```

time: 86 us -> 59.2 us (0.69); the launches traced: 84.6 us -> 59 us
  Pallas kernels: 79.4 us -> 56.7 us
  local copies, waits for them, and re-layouts: 4.45 us -> 1.67 us
    pallas_call x1, Pallas kernels: 79.4 us -> 56.7 us  [body(): pl.pallas_call(kernel, out_shape=pltpu.VMEM(queries.shape, jnp.bfloat16),...]
    unnamed x1, local copies, waits for them, and re-layouts: 3.97 us -> 1.67 us
where the time goes in v1:
time: 59.2 us; the launch traced here: 59 us
  Pallas kernels  56.7 us (96%)
  local copies, waits for them, and re-layouts  1.67 us (3%)
  between operations  0.66 us (1%)
    pallas_call x1, Pallas kernels, body(): pl.pallas_call(kernel, out_shape=pltpu.VMEM(queries.shape, jnp.bfloat16),...  56.7 us
    unnamed x1, local copies, waits for them, and re-layouts  1.67 us

profile of v1, /device:TPU:16, one launch (start us, length us, event | category | flops | bytes accessed | tf_op | source)
XLA Modules:
  0.0 59.0 jit_solution(17959803403076668594)
XLA Ops:
  0.7 56.7 %shard_map.46 = bf16[768,2048]{1,0:T(8,128)(2,1)S(1)} custom-call(s32[1]{0:T(128)S(6)} %copy.7.lens_ref, bf16[768,2048]{1,0:T(8,128)(2,1)} %q_ref.1, bf16[768,256]{1,0:T(8,128)(2,1)} %k_ref.1, bf16[768,256]{1,0:T(8,128)(2,1)} %v_ref.1), custom_call_target="tpu_custom_call" | custom-call | tf_op jit(solution)/shard_map/pallas_call | solution.py:432
  57.3 1.7 %copy.6 = bf16[768,2048]{1,0:T(8,128)(2,1)} copy(bf16[768,2048]{1,0:T(8,128)(2,1)S(1)} %shard_map.46) | data formatting | bytes 6291456

commit v2 on v1

--- a/solution.py
+++ b/solution.py
@@ -47,8 +47,7 @@
     p_buf,
     m_now,
     shrink,
-    lens_send,
-    lens_recv,
+    lens_sems,
     in_sems,
     q_sems,
     send_sems,
@@ -116,8 +115,8 @@
         return pltpu.make_async_remote_copy(
             src_ref=lens.at[pl.ds(slot * per, per)],
             dst_ref=lens.at[pl.ds(slot * per, per)],
-            send_sem=lens_send.at[i],
-            recv_sem=lens_recv.at[slot],
+            send_sem=lens_sems.at[0],
+            recv_sem=lens_sems.at[1],
             device_id=peer(offsets[i]),
             device_id_type=MESH,
         )
@@ -129,7 +128,7 @@
         return pltpu.make_async_remote_copy(
             src_ref=place(rel_here, j),
             dst_ref=place(rel_there, j),
-            send_sem=send_sems.at[kind, j],
+            send_sem=send_sems.at[kind],
             recv_sem=recv_sems.at[rel_there, j],
             device_id=(to, head),
             device_id_type=MESH,
@@ -201,9 +200,18 @@
 
     lax.fori_loop(0, pieces, turn, 0)
 
-    for i in range(count - 1):
-        there = peer(offsets[i])
-        lens_copy(there[0] * n_head + there[1], i).wait_recv()
+    def all_lens():
+        others = lens.at[pl.ds(0, (count - 1) * per)]
+        return pltpu.make_async_remote_copy(
+            src_ref=others,
+            dst_ref=others,
+            send_sem=lens_sems.at[0],
+            recv_sem=lens_sems.at[1],
+            device_id=peer(offsets[0]),
+            device_id_type=MESH,
+        )
+
+    all_lens().wait_recv()
 
     n_groups = digit_a.shape[0]
     position = (
@@ -410,11 +418,17 @@
     for kind, here, there, chunks, to, condition in sends:
         @pl.when(condition)
         def _():
-            for j in chunks:
-                hop(kind, here, there, j, to).wait_send()
-
-    for i in range(count - 1):
-        lens_copy(me, i).wait_send()
+            sent = kv.at[pl.ds(0, len(chunks) * TILE), :]
+            pltpu.make_async_remote_copy(
+                src_ref=sent,
+                dst_ref=sent,
+                send_sem=send_sems.at[kind],
+                recv_sem=recv_sems.at[0, 0],
+                device_id=(to, head),
+                device_id_type=MESH,
+            ).wait_send()
+
+    all_lens().wait_send()
 
 
 def body(n_seq, n_head, doc_lengths, queries, key_states, value_states):
@@ -450,11 +464,10 @@
             pltpu.VMEM((PS, rows, CHUNK), jnp.bfloat16),
             pltpu.VMEM((units, 1, CHUNK), jnp.float32),
             pltpu.VMEM((units, 1, CHUNK), jnp.float32),
-            pltpu.SemaphoreType.DMA((count,)),
-            pltpu.SemaphoreType.DMA((count,)),
+            pltpu.SemaphoreType.DMA((2,)),
             pltpu.SemaphoreType.DMA((2,)),
             pltpu.SemaphoreType.DMA((pieces,)),
-            pltpu.SemaphoreType.DMA((9, pieces)),
+            pltpu.SemaphoreType.DMA((9,)),
             pltpu.SemaphoreType.DMA((back + 1, pieces)),
         ],
         compiler_params=pltpu.CompilerParams(

time: 59.2 us -> 58.1 us (0.981)
  Pallas kernels: 56.7 us -> 55.6 us
    pallas_call x1, Pallas kernels: 56.7 us -> 55.6 us  [body(): pl.pallas_call(kernel, out_shape=pltpu.VMEM(queries.shape, jnp.bfloat16),...]
where the time goes in v2:
time: 58.1 us; the launch traced here: 58 us
  Pallas kernels  55.6 us (96%)
  local copies, waits for them, and re-layouts  1.67 us (3%)
  between operations  0.66 us (1%)
    pallas_call x1, Pallas kernels, body(): pl.pallas_call(kernel, out_shape=pltpu.VMEM(queries.shape, jnp.bfloat16),...  55.6 us
    unnamed x1, local copies, waits for them, and re-layouts  1.67 us

profile of v2, /device:TPU:16, one launch (start us, length us, event | category | flops | bytes accessed | tf_op | source)
XLA Modules:
  0.0 58.0 jit_solution(11444814988105292426)
XLA Ops:
  0.7 55.6 %shard_map.46 = bf16[768,2048]{1,0:T(8,128)(2,1)S(1)} custom-call(s32[1]{0:T(128)S(6)} %copy.7.lens_ref, bf16[768,2048]{1,0:T(8,128)(2,1)} %q_ref.1, bf16[768,256]{1,0:T(8,128)(2,1)} %k_ref.1, bf16[768,256]{1,0:T(8,128)(2,1)} %v_ref.1), custom_call_target="tpu_custom_call" | custom-call | tf_op jit(solution)/shard_map/pallas_call | solution.py:446
  56.3 1.7 %copy.6 = bf16[768,2048]{1,0:T(8,128)(2,1)} copy(bf16[768,2048]{1,0:T(8,128)(2,1)S(1)} %shard_map.46) | data formatting | bytes 6291456
